TPU v7x, 32 devices: a whole 2x2x4 slice. The times are simulated.
32 devices in a mesh: depth: 4 (over z), rows: 8 (over y, x, core).
Axes of the slice: x: 2, y: 2, z: 4, core: 2. Of those that a mesh axis runs over, the one named last changes fastest.
Arguments:
- target: float32 [4, 2, 4096, 4096], P('depth', None, 'rows'), may hold values from -6 to 6
- depth_index: int32 [4], P('depth'), may hold values from 0 to 255
- band_mask: int32 [4, 2, 4096], P('depth'), may hold values from 0 to 1, as said below
Outputs:
- hologram: float32 [2, 4096, 4096], P(None, ('depth', 'rows'))
Inputs may be any that keep to these rules, and one draw needn't show every extreme that they name: `band_mask`: for each plane and each of the two dimensions, the ones are exactly the frequency indices k with min(k, 4096 - k) below a cutoff between 512 and 2048.
All inputs are finite; a program needn't handle non-finite values.
Results may differ from a plain program's by a relative error of at most 0.0009.
Values sent between devices are 32-bit elements; how exact they have to be, the bound alone decides.
A program may use at most 128 MiB of HBM per device.

v0:
```python
import math
import jax
import jax.numpy as jnp
from jax import lax
from jax.sharding import PartitionSpec as P

LOW = 32
HIGH = 128
N = 4096
precise = lax.Precision.HIGHEST


def block_table(length, direction):
    indices = jnp.arange(length, dtype=jnp.int32)
    product = indices[:, None] * indices[None, :] % length
    angles = direction * 2.0 * math.pi / length * product.astype(jnp.float32)
    cosine = jnp.cos(angles)
    sine_part = jnp.sin(angles)
    upper_rows = jnp.stack([cosine, -sine_part], axis=1)
    lower_rows = jnp.stack([sine_part, cosine], axis=1)
    return jnp.stack([upper_rows, lower_rows], axis=0)


def twiddles(direction):
    first = jnp.arange(LOW, dtype=jnp.int32)
    second = jnp.arange(HIGH, dtype=jnp.int32)
    product = first[:, None] * second[None, :] % N
    angles = direction * 2.0 * math.pi / N * product.astype(jnp.float32)
    scaling = 1.0 / math.sqrt(N)
    return (jnp.cos(angles) * scaling, jnp.sin(angles) * scaling)


def rotate_pair(data, factor_real, factor_imaginary, comp_axis):
    real_part = jnp.take(data, 0, axis=comp_axis)
    imaginary_part = jnp.take(data, 1, axis=comp_axis)
    return jnp.stack(
        [
            real_part * factor_real - imaginary_part * factor_imaginary,
            real_part * factor_imaginary + imaginary_part * factor_real,
        ],
        axis=comp_axis,
    )


def along_width(planes):
    plane_count, _, height, _ = planes.shape
    factor_real, factor_imaginary = twiddles(-1.0)
    pieces = planes.reshape(plane_count, 2, height, LOW, HIGH)
    sectioned = jnp.einsum("akbn,pbrnm->parkm", block_table(LOW, -1.0), pieces, precision=precise)
    turned = rotate_pair(sectioned, factor_real, factor_imaginary, 1)
    result = jnp.einsum("akbn,pbrjn->parjk", block_table(HIGH, -1.0), turned, precision=precise)
    return result.reshape(plane_count, 2, height, N)


def along_height(columns):
    plane_count, _, _, slab_width = columns.shape
    factor_real, factor_imaginary = twiddles(-1.0)
    pieces = columns.reshape(plane_count, 2, LOW, HIGH, slab_width)
    sectioned = jnp.einsum("akbn,pbnjs->pakjs", block_table(LOW, -1.0), pieces, precision=precise)
    turned = rotate_pair(sectioned, factor_real[:, :, None], factor_imaginary[:, :, None], 1)
    result = jnp.einsum("akbn,pbjns->pajks", block_table(HIGH, -1.0), turned, precision=precise)
    return result.reshape(plane_count, 2, N, slab_width)


def inverse_height(spectrum):
    slab_width = spectrum.shape[2]
    factor_real, factor_imaginary = twiddles(1.0)
    pieces = spectrum.reshape(2, LOW, HIGH, slab_width)
    sectioned = jnp.einsum("anbk,bjks->ajns", block_table(HIGH, 1.0), pieces, precision=precise)
    turned = rotate_pair(sectioned, factor_real[:, :, None], factor_imaginary[:, :, None], 0)
    result = jnp.einsum("anbk,bkjs->anjs", block_table(LOW, 1.0), turned, precision=precise)
    return result.reshape(2, N, slab_width)


def inverse_width(row_block):
    height = row_block.shape[1]
    factor_real, factor_imaginary = twiddles(1.0)
    pieces = row_block.reshape(2, height, LOW, HIGH)
    sectioned = jnp.einsum("anbk,byjk->ayjn", block_table(HIGH, 1.0), pieces, precision=precise)
    turned = rotate_pair(sectioned, factor_real, factor_imaginary, 0)
    result = jnp.einsum("anbk,bykj->aynj", block_table(LOW, 1.0), turned, precision=precise)
    return result.reshape(2, height, N)


def frequencies(ordering):
    first = ordering // HIGH
    second = ordering % HIGH
    natural = first + LOW * second
    signed = jnp.where(natural < N // 2, natural, natural - N)
    return signed.astype(jnp.float32) / N


def reorder_mask(band_mask):
    leading = band_mask.shape[:-1]
    grid = band_mask.reshape(leading + (HIGH, LOW))
    return jnp.swapaxes(grid, -1, -2).reshape(leading + (N,))


def local(target, depth_index, band_mask):
    plane_count = target.shape[0]
    spectra_width = along_width(target)
    columns = along_height(
        lax.all_to_all(spectra_width, "rows", split_axis=3, concat_axis=2, tiled=True)
    )
    slab_width = columns.shape[3]
    offset = lax.axis_index("rows") * slab_width
    freq_height = frequencies(jnp.arange(N, dtype=jnp.int32))
    freq_width = frequencies(offset + jnp.arange(slab_width, dtype=jnp.int32))
    radical = jnp.sqrt(4.0 - freq_height[:, None] ** 2 - freq_width[None, :] ** 2)
    distance = 100.0 + 2.0 * depth_index.astype(jnp.float32)
    phases = (2.0 * math.pi * distance)[:, None, None] * (radical - 2.0)[None, :, :]
    ordered = reorder_mask(band_mask)
    mask_height = ordered[:, 0, :].astype(jnp.float32)
    mask_width = lax.dynamic_slice_in_dim(ordered[:, 1, :], offset, slab_width, 1).astype(
        jnp.float32
    )
    weights = mask_height[:, :, None] * mask_width[:, None, :]
    cosine = jnp.cos(phases) * weights
    sine_part = jnp.sin(phases) * weights
    real_part = columns[:, 0]
    imaginary_part = columns[:, 1]
    spectrum = jnp.stack(
        [
            jnp.sum(real_part * cosine - imaginary_part * sine_part, axis=0),
            jnp.sum(real_part * sine_part + imaginary_part * cosine, axis=0),
        ]
    )
    scaling = 1.0 / math.sqrt(plane_count * lax.axis_size("depth"))
    field_part = inverse_height(spectrum)
    shares = lax.psum_scatter(field_part, "depth", scatter_dimension=1, tiled=True)
    rows_out = lax.all_to_all(shares, "rows", split_axis=1, concat_axis=2, tiled=True)
    return inverse_width(rows_out) * scaling


def solution(mesh):
    in_specs = (P("depth", None, "rows", None), P("depth"), P("depth", None, None))
    out_specs = P(None, ("depth", "rows"), None)
    return jax.shard_map(local, mesh=mesh, in_specs=in_specs, out_specs=out_specs, check_vma=False)
```

profile of v0, /device:TPU:0, one launch (start us, length us, event | category | flops | bytes accessed | tf_op | source)
XLA Modules:
  0.0 982.7 jit_solution(7739893141141795553)
XLA Ops:
  6.5 0.1 multiply_sine_fusion.2
  6.7 0.1 sine_multiply_fusion.1
  6.8 0.3 multiply_sine_fusion.1
  7.1 0.3 fusion.49
  7.3 14.1 %copy.117 = f32[128,8,32,128]{3,2,1,0:T(8,128)} copy(f32[128,8,32,128]{3,1,2,0:T(8,128)} %bitcast.227) | data formatting | bytes 33554432
  21.4 22.1 %fusion.24 = f32[1,2,512,32,128]{4,3,2,1,0:T(8,128)} fusion(f32[1,32,2,32]{3,1,2,0:T(8,128)S(1)} %get-tuple-element.122, f32[1,32,2,32]{3,1,2,0:T(8,128)S(1)} %get-tuple-element.121, f32[2,512,32,128]{3,2,1,0:T(8,128)} %bitcast.219), kind=kOutput, calls=%fused_computation.39 | convolution fusion | flops 3221229568 | bytes 33570816 | tf_op jit(solution)/shard_map/akbn,pbrnm->parkm/dot_general | solution.py:49
  43.6 7.2 subtract_bitcast_fusion.2
  50.7 6.2 maximum_bitcast_fusion
  56.9 42.9 %fusion.14 = f32[1,2,512,32,128]{2,4,1,3,0:T(8,128)} fusion(f32[2,512,32,128,1]{3,2,1,0,4:T(8,128)} %maximum_bitcast_fusion, f32[1,128,2,128]{3,1,2,0:T(8,128)S(1)} %get-tuple-element.116, f32[1,128,2,128]{3,1,2,0:T(8,128)S(1)} %get-tuple-element.115), kind=kOutput, calls=%fused_computation.20 | convolution fusion | flops 12884967424 | bytes 33816576 | tf_op jit(solution)/shard_map/akbn,pbrjn->parjk/dot_general | solution.py:51
  99.9 6.9 copy.63
  106.7 32.2 %copy.64 = f32[1,2,512,4096]{2,1,0,3:T(2,128)} copy(f32[1,2,512,4096]{2,3,1,0:T(8,128)S(1)} %bitcast.223) | data formatting | bytes 33554432 | tf_op jit(solution)/shard_map/reshape | solution.py:52
  139.0 5.9 all-to-all-start
  144.9 0.1 copy.69
  145.0 0.1 copy.70
  145.1 0.1 reshape.712
  146.2 0.1 sine_multiply_fusion
  146.3 0.1 multiply_sine_fusion.3
  146.3 0.3 fusion.50
  146.6 0.3 multiply_sine_fusion
  146.9 182.5 %all-to-all-done = f32[1,2,512,4096]{2,1,0,3:T(2,128)} async-done(((f32[1,2,512,4096]{2,1,0,3:T(2,128)}), f32[1,2,512,4096]{2,1,0,3:T(2,128)}, u32[]{:S(2)}, u32[]{:S(2)}) %all-to-all-start) | async-done | bytes 16777248 | tf_op jit(solution)/shard_map/all_to_all | solution.py:103
  329.4 14.1 %copy.65 = f32[1,2,512,4096]{2,3,1,0:T(8,128)} copy(f32[1,2,512,4096]{2,1,0,3:T(2,128)} %all-to-all-done) | data formatting | bytes 33554432 | tf_op jit(solution)/shard_map/all_to_all | solution.py:103
  343.5 17.3 %copy.66 = f32[1,2,8,512,512]{4,3,2,1,0:T(8,128)} copy(f32[1,2,8,512,512]{3,4,2,1,0:T(8,128)} %bitcast.224) | data formatting | bytes 33554432 | tf_op jit(solution)/shard_map/all_to_all | solution.py:103
  360.8 32.4 %fusion.17 = f32[1,2,32,128,512]{4,2,1,3,0:T(8,128)S(1)} fusion(f32[2,32,128,512,1]{3,2,1,0,4:T(8,128)} %bitcast.220, f32[1,32,2,32]{3,1,2,0:T(8,128)S(1)} %get-tuple-element.122, f32[1,32,2,32]{3,1,2,0:T(8,128)S(1)} %get-tuple-element.121), kind=kOutput, calls=%fused_computation.21 | convolution fusion | flops 3221229568 | bytes 33570816 | tf_op jit(solution)/shard_map/akbn,pbnjs->pakjs/dot_general | solution.py:59
  393.2 4.5 subtract_bitcast_fusion.1
  397.7 4.9 maximum_bitcast_fusion.1
  402.6 27.0 %fusion.20 = f32[1,2,32,128,512]{4,3,1,2,0:T(8,128)S(1)} fusion(f32[2,32,128,512,1]{3,1,2,0,4:T(8,128)S(1)} %maximum_bitcast_fusion.1, f32[1,128,2,128]{3,1,2,0:T(8,128)S(1)} %get-tuple-element.116, f32[1,128,2,128]{3,1,2,0:T(8,128)S(1)} %get-tuple-element.115), kind=kOutput, calls=%fused_computation.22 | convolution fusion | flops 12884967424 | bytes 33816576 | tf_op jit(solution)/shard_map/akbn,pbjns->pajks/dot_general | solution.py:61
  429.6 6.2 copy.72
  435.8 10.9 %fusion.86 = (f32[1,1,4096,512]{3,2,1,0:T(8,128)}, f32[1,1,4096,512]{3,2,1,0:T(8,128)}) fusion(f32[1,2,4096,512]{3,2,1,0:T(8,128)} %bitcast.222), kind=kLoop, calls=%fused_computation.148 | loop fusion | bytes 33554432 | tf_op jit(solution)/shard_map/slice | solution.py:120
  446.7 9.0 copy.74
  455.7 9.0 copy.75
  464.7 37.7 %multiply_subtract_fusion = (f32[1,32,128,512]{2,3,0,1:T(8,128)S(1)}, f32[1,32,128,512]{2,3,0,1:T(8,128)}) fusion(f32[1,32,128,512]{2,3,0,1:T(8,128)} %copy.75, f32[1,32,128,512]{2,3,0,1:T(8,128)} %copy.74, f32[512]{0:T(512)S(1)} %bitcast.233, f32[32,128]{1,0:T(8,128)S(1)} %bitcast.232, f32[512]{0:T(512)S(1)} %multiply_multiply_fusion.2, ...), kind=kLoop, calls=%fused_computation.33 | loop fusion | flops 25165824 | bytes 33591300 | tf_op jit(solution)/shard_map/sub | solution.py:124
  502.4 16.5 %fusion.23 = f32[2,32,128,512]{2,3,0,1:T(8,128)S(1)} fusion(f32[1,32,128,512]{2,3,0,1:T(8,128)} %get-tuple-element.104, f32[1,32,128,512]{2,3,0,1:T(8,128)S(1)} %get-tuple-element.103, f32[1,128,2,128]{3,1,2,0:T(8,128)S(1)} %get-tuple-element.114, f32[1,128,2,128]{3,1,2,0:T(8,128)S(1)} %get-tuple-element.113), kind=kOutput, calls=%fused_computation.23 | convolution fusion | flops 12889161728 | bytes 33816576 | tf_op jit(solution)/shard_map/anbk,bjks->ajns/dot_general | solution.py:69
  518.9 6.9 subtract_bitcast_fusion
  525.8 11.5 %pad_maximum_fusion = f32[2,32,128,512]{2,3,1,0:T(8,128)} fusion(f32[1,32,128,512]{2,3,1,0:T(8,128)} %get-tuple-element.106, f32[1,32,128,512]{2,3,1,0:T(8,128)} %get-tuple-element.105), kind=kLoop, calls=%fused_computation.6 | loop fusion | flops 4194304 | bytes 33554432 | tf_op jit(solution)/shard_map/stack | solution.py:36
  537.3 19.9 %copy.79 = f32[2,32,128,512]{3,1,0,2:T(8,128)} copy(f32[2,32,128,512]{2,3,1,0:T(8,128)} %pad_maximum_fusion) | data formatting | bytes 33554432 | tf_op jit(solution)/shard_map/stack | solution.py:36
  557.2 21.8 %fusion.27 = f32[2,32,128,512]{3,1,2,0:T(8,128)} fusion(f32[2,32,128,512]{3,1,0,2:T(8,128)} %copy.79, f32[1,32,2,32]{3,1,2,0:T(8,128)S(1)} %get-tuple-element.120, f32[1,32,2,32]{3,1,2,0:T(8,128)S(1)} %get-tuple-element.119), kind=kOutput, calls=%fused_computation.40 | convolution fusion | flops 3221229568 | bytes 33570816 | tf_op jit(solution)/shard_map/anbk,bkjs->anjs/dot_general | solution.py:71
  579.0 17.9 %copy.80 = f32[2,32,128,512]{3,2,1,0:T(8,128)} copy(f32[2,32,128,512]{3,1,2,0:T(8,128)} %fusion.27) | data formatting | bytes 33554432 | tf_op jit(solution)/shard_map/anbk,bkjs->anjs/dot_general | solution.py:71
  596.9 280.8 %reduce-scatter.2.cloned.1.call-done = f32[2,1024,512]{2,1,0:T(8,128)} async-done(((f32[2,4096,512]{2,1,0:T(8,128)}), f32[2,1024,512]{2,1,0:T(8,128)}) %reduce-scatter.2.cloned.1.call-update) | async-done | bytes 4194320 | tf_op jit(solution)/shard_map/reduce_scatter | solution.py:130
  877.7 5.4 copy.81
  883.1 52.5 %all_to_all.30 = f32[2,1024,512]{2,0,1:T(2,128)S(1)} all-to-all(f32[2,1024,512]{2,0,1:T(2,128)S(1)} %copy.81), channel_id=1, replica_groups=mesh['depth'=4,'rows'=8] {'rows'}, dimensions={1} | all-to-all | bytes 8388608 | tf_op jit(solution)/shard_map/all_to_all | solution.py:131
  935.6 2.8 copy.82
  938.4 5.3 copy.83
  943.8 8.5 fusion.35
  952.3 0.9 subtract_bitcast_fusion.3
  953.2 0.5 maximum_bitcast_fusion.6
  953.7 9.0 fusion.30
  962.7 6.0 mul.976
  968.8 6.6 copy.87
  (15 shorter events, 0.4 us)
Async XLA Ops:
  139.0 6.1 copy-start
  139.0 190.5 %all-to-all-start = ((f32[1,2,512,4096]{2,1,0,3:T(2,128)}), f32[1,2,512,4096]{2,1,0,3:T(2,128)}, u32[]{:S(2)}, u32[]{:S(2)}) async-start(f32[1,2,512,4096]{2,1,0,3:T(2,128)} %copy.64), calls=%async_computation | async-start | bytes 33554432 | tf_op jit(solution)/shard_map/all_to_all | solution.py:103
  144.9 732.9 %reduce-scatter.2.cloned.1.call-start = ((), (), s32[]{:S(2)}) async-start(), calls=%async_computation.3 | async-start | bytes 20971520 | tf_op jit(solution)/shard_map/reduce_scatter | solution.py:130
Sparse Core Ops, SparseCore 0:
  597.0 280.6 reduce-scatter.1
where the time goes:
time: 993 us; the launch traced here: 983 us
  waiting for transfers between devices  463 us (47%)
  local copies, waits for them, and re-layouts  184 us (19%)
  matrix products  180 us (18%)
  other arithmetic  81.9 us (8%)
  blocking collectives  52.5 us (5%)
  between operations  14.7 us (1%)
    reduce_scatter x1, waiting for transfers between devices, local(): lax.psum_scatter(field_part, 'depth', scatter_dimension=1, tiled=True)  281 us
    all_to_all x1, waiting for transfers between devices, local(): lax.all_to_all(spectra_width, 'rows', split_axis=3, concat_axis=2, tiled=...  183 us
    all_to_all x1, blocking collectives, local(): lax.all_to_all(shares, 'rows', split_axis=1, concat_axis=2, tiled=True)  52.5 us
    dot_general x1, matrix products, along_width(): jnp.einsum('akbn,pbrjn->parjk', block_table(HIGH, -1.0), turned, precisio...  42.9 us
    sub x1, other arithmetic, local(): real_part * cosine - imaginary_part * sine_part  37.7 us
    dot_general x1, matrix products, along_height(): jnp.einsum('akbn,pbnjs->pakjs', block_table(LOW, -1.0), pieces, precision...  32.4 us
    reshape x1, local copies, waits for them, and re-layouts, along_width(): return result.reshape(plane_count, 2, height, N)  32.2 us
    another operation x6, other arithmetic, rotate_pair(): jnp.stack([real_part * factor_real - imaginary_part * factor_imaginary, r...  31.4 us
  transfers between devices with their start and end apart: 2, of which 2 were waited for; matrix products, arithmetic and copies ran while one was open for 0% of the time, Pallas kernels for 0%

commit v1 on v0

--- a/solution.py
+++ b/solution.py
@@ -100,7 +100,12 @@
     plane_count = target.shape[0]
     spectra_width = along_width(target)
     columns = along_height(
-        lax.all_to_all(spectra_width, "rows", split_axis=3, concat_axis=2, tiled=True)
+        jnp.concatenate(
+            lax.all_to_all(
+                jnp.stack(jnp.split(spectra_width, lax.axis_size("rows"), axis=3)), "rows", 0, 0
+            ),
+            axis=2,
+        )
     )
     slab_width = columns.shape[3]
     offset = lax.axis_index("rows") * slab_width

time: 993 us -> 950 us (0.957)
  local copies, waits for them, and re-layouts: 184 us -> 151 us
    all_to_all x2 -> x0, local copies, waits for them, and re-layouts: 31.4 us -> none  [local(): lax.all_to_all(spectra_width, 'rows', split_axis=3, concat_axis=2, tiled=...]
    reshape x1, local copies, waits for them, and re-layouts: 32.2 us -> 17.6 us  [local(): jnp.concatenate(lax.all_to_all(jnp.stack(jnp.split(spectra_width, lax.axi...]
    unnamed x3 -> x10, local copies, waits for them, and re-layouts: 14.1 us -> 24.7 us
where the time goes in v1:
time: 950 us; the launch traced here: 940 us
  waiting for transfers between devices  463 us (49%)
  matrix products  171 us (18%)
  local copies, waits for them, and re-layouts  151 us (16%)
  other arithmetic  81.9 us (9%)
  blocking collectives  52.5 us (6%)
  between operations  14.7 us (2%)
    reduce_scatter x1, waiting for transfers between devices, local(): lax.psum_scatter(field_part, 'depth', scatter_dimension=1, tiled=True)  281 us
    all_to_all x1, waiting for transfers between devices, local(): lax.all_to_all(jnp.stack(jnp.split(spectra_width, lax.axis_size('rows'),...  183 us
    all_to_all x1, blocking collectives, local(): lax.all_to_all(shares, 'rows', split_axis=1, concat_axis=2, tiled=True)  52.5 us
    sub x1, other arithmetic, local(): real_part * cosine - imaginary_part * sine_part  37.7 us
    dot_general x1, matrix products, along_width(): jnp.einsum('akbn,pbrjn->parjk', block_table(HIGH, -1.0), turned, precisio...  33.2 us
    dot_general x1, matrix products, along_height(): jnp.einsum('akbn,pbnjs->pakjs', block_table(LOW, -1.0), pieces, precision...  32.4 us
    another operation x6, other arithmetic, rotate_pair(): jnp.stack([real_part * factor_real - imaginary_part * factor_imaginary, r...  31.4 us
    dot_general x1, matrix products, along_height(): jnp.einsum('akbn,pbjns->pajks', block_table(HIGH, -1.0), turned, precisio...  27 us
  transfers between devices with their start and end apart: 2, of which 2 were waited for; matrix products, arithmetic and copies ran while one was open for 0% of the time, Pallas kernels for 0%

profile of v1, /device:TPU:0, one launch (start us, length us, event | category | flops | bytes accessed | tf_op | source)
XLA Modules:
  0.0 939.6 jit_solution(18001811838296417870)
XLA Ops:
  6.8 0.3 multiply_sine_fusion.1
  7.1 0.3 fusion.57
  7.3 14.1 %copy.115 = f32[128,8,32,128]{3,2,1,0:T(8,128)} copy(f32[128,8,32,128]{3,1,2,0:T(8,128)} %bitcast.263) | data formatting | bytes 33554432
  21.4 22.1 %fusion.24 = f32[1,2,512,32,128]{4,3,2,1,0:T(8,128)} fusion(f32[1,32,2,32]{3,1,2,0:T(8,128)S(1)} %get-tuple-element.122, f32[1,32,2,32]{3,1,2,0:T(8,128)S(1)} %get-tuple-element.121, f32[2,512,32,128]{3,2,1,0:T(8,128)} %bitcast.249), kind=kOutput, calls=%fused_computation.39 | convolution fusion | flops 3221229568 | bytes 33570816 | tf_op jit(solution)/shard_map/akbn,pbrnm->parkm/dot_general | solution.py:49
  43.6 7.2 subtract_bitcast_fusion.2
  50.7 6.2 maximum_bitcast_fusion
  56.9 33.2 %fusion.14 = f32[1,2,512,32,128]{2,4,1,3,0:T(8,128)} fusion(f32[2,512,32,128,1]{3,2,1,0,4:T(8,128)} %maximum_bitcast_fusion, f32[1,128,2,128]{3,1,2,0:T(8,128)S(1)} %get-tuple-element.116, f32[1,128,2,128]{3,1,2,0:T(8,128)S(1)} %get-tuple-element.115), kind=kOutput, calls=%fused_computation.20 | convolution fusion | flops 12884967424 | bytes 33816576 | tf_op jit(solution)/shard_map/akbn,pbrjn->parjk/dot_general | solution.py:51
  90.2 7.4 copy.63
  97.6 1.5 fusion.47
  99.1 1.5 fusion.46
  100.6 1.5 fusion.45
  102.1 1.5 fusion.44
  103.6 1.6 fusion.43
  105.2 1.5 fusion.42
  106.7 1.5 fusion.41
  108.2 1.5 fusion.40
  109.7 5.9 all-to-all-start
  115.8 0.1 reshape.714
  117.0 0.3 fusion.58
  117.3 0.3 multiply_sine_fusion
  117.6 182.5 %all-to-all-done = f32[8,1,2,512,512]{3,4,2,1,0:T(8,128)} async-done(((f32[8,1,2,512,512]{3,4,2,1,0:T(8,128)}), f32[8,1,2,512,512]{3,4,2,1,0:T(8,128)}, u32[]{:S(2)}, u32[]{:S(2)}) %all-to-all-start) | async-done | bytes 16777248 | tf_op jit(solution)/shard_map/all_to_all | solution.py:104
  300.1 17.6 %copy.64 = f32[1,2,8,512,512]{4,3,2,1,0:T(8,128)} copy(f32[1,2,8,512,512]{3,4,1,0,2:T(8,128)} %bitcast.39) | data formatting | bytes 33554432 | tf_op jit(solution)/shard_map/reshape | solution.py:103
  317.7 32.4 %fusion.17 = f32[1,2,32,128,512]{4,2,1,3,0:T(8,128)S(1)} fusion(f32[2,32,128,512,1]{3,2,1,0,4:T(8,128)} %bitcast.250, f32[1,32,2,32]{3,1,2,0:T(8,128)S(1)} %get-tuple-element.122, f32[1,32,2,32]{3,1,2,0:T(8,128)S(1)} %get-tuple-element.121), kind=kOutput, calls=%fused_computation.21 | convolution fusion | flops 3221229568 | bytes 33570816 | tf_op jit(solution)/shard_map/akbn,pbnjs->pakjs/dot_general | solution.py:59
  350.1 4.5 subtract_bitcast_fusion.1
  354.6 4.9 maximum_bitcast_fusion.1
  359.5 27.0 %fusion.20 = f32[1,2,32,128,512]{4,3,1,2,0:T(8,128)S(1)} fusion(f32[2,32,128,512,1]{3,1,2,0,4:T(8,128)S(1)} %maximum_bitcast_fusion.1, f32[1,128,2,128]{3,1,2,0:T(8,128)S(1)} %get-tuple-element.116, f32[1,128,2,128]{3,1,2,0:T(8,128)S(1)} %get-tuple-element.115), kind=kOutput, calls=%fused_computation.22 | convolution fusion | flops 12884967424 | bytes 33816576 | tf_op jit(solution)/shard_map/akbn,pbjns->pajks/dot_general | solution.py:61
  386.5 6.2 copy.70
  392.7 10.9 %fusion.94 = (f32[1,1,4096,512]{3,2,1,0:T(8,128)}, f32[1,1,4096,512]{3,2,1,0:T(8,128)}) fusion(f32[1,2,4096,512]{3,2,1,0:T(8,128)} %bitcast.260), kind=kLoop, calls=%fused_computation.164 | loop fusion | bytes 33554432 | tf_op jit(solution)/shard_map/slice | solution.py:125
  403.6 9.0 copy.72
  412.6 9.0 copy.73
  421.6 37.7 %multiply_subtract_fusion = (f32[1,32,128,512]{2,3,0,1:T(8,128)S(1)}, f32[1,32,128,512]{2,3,0,1:T(8,128)}) fusion(f32[1,32,128,512]{2,3,0,1:T(8,128)} %copy.73, f32[1,32,128,512]{2,3,0,1:T(8,128)} %copy.72, f32[512]{0:T(512)S(1)} %bitcast.269, f32[32,128]{1,0:T(8,128)S(1)} %bitcast.268, f32[512]{0:T(512)S(1)} %multiply_multiply_fusion.2, ...), kind=kLoop, calls=%fused_computation.33 | loop fusion | flops 25165824 | bytes 33591300 | tf_op jit(solution)/shard_map/sub | solution.py:129
  459.3 16.5 %fusion.23 = f32[2,32,128,512]{2,3,0,1:T(8,128)S(1)} fusion(f32[1,32,128,512]{2,3,0,1:T(8,128)} %get-tuple-element.104, f32[1,32,128,512]{2,3,0,1:T(8,128)S(1)} %get-tuple-element.103, f32[1,128,2,128]{3,1,2,0:T(8,128)S(1)} %get-tuple-element.114, f32[1,128,2,128]{3,1,2,0:T(8,128)S(1)} %get-tuple-element.113), kind=kOutput, calls=%fused_computation.23 | convolution fusion | flops 12889161728 | bytes 33816576 | tf_op jit(solution)/shard_map/anbk,bjks->ajns/dot_general | solution.py:69
  475.8 6.9 subtract_bitcast_fusion
  482.7 11.5 %pad_maximum_fusion = f32[2,32,128,512]{2,3,1,0:T(8,128)} fusion(f32[1,32,128,512]{2,3,1,0:T(8,128)} %get-tuple-element.106, f32[1,32,128,512]{2,3,1,0:T(8,128)} %get-tuple-element.105), kind=kLoop, calls=%fused_computation.6 | loop fusion | flops 4194304 | bytes 33554432 | tf_op jit(solution)/shard_map/stack | solution.py:36
  494.2 19.9 %copy.77 = f32[2,32,128,512]{3,1,0,2:T(8,128)} copy(f32[2,32,128,512]{2,3,1,0:T(8,128)} %pad_maximum_fusion) | data formatting | bytes 33554432 | tf_op jit(solution)/shard_map/stack | solution.py:36
  514.1 21.8 %fusion.27 = f32[2,32,128,512]{3,1,2,0:T(8,128)} fusion(f32[2,32,128,512]{3,1,0,2:T(8,128)} %copy.77, f32[1,32,2,32]{3,1,2,0:T(8,128)S(1)} %get-tuple-element.120, f32[1,32,2,32]{3,1,2,0:T(8,128)S(1)} %get-tuple-element.119), kind=kOutput, calls=%fused_computation.40 | convolution fusion | flops 3221229568 | bytes 33570816 | tf_op jit(solution)/shard_map/anbk,bkjs->anjs/dot_general | solution.py:71
  535.9 17.9 %copy.78 = f32[2,32,128,512]{3,2,1,0:T(8,128)} copy(f32[2,32,128,512]{3,1,2,0:T(8,128)} %fusion.27) | data formatting | bytes 33554432 | tf_op jit(solution)/shard_map/anbk,bkjs->anjs/dot_general | solution.py:71
  553.8 280.8 %reduce-scatter.2.cloned.1.call-done = f32[2,1024,512]{2,1,0:T(8,128)} async-done(((f32[2,4096,512]{2,1,0:T(8,128)}), f32[2,1024,512]{2,1,0:T(8,128)}) %reduce-scatter.2.cloned.1.call-update) | async-done | bytes 4194320 | tf_op jit(solution)/shard_map/reduce_scatter | solution.py:135
  834.6 5.4 copy.79
  840.0 52.5 %all_to_all.20 = f32[2,1024,512]{2,0,1:T(2,128)S(1)} all-to-all(f32[2,1024,512]{2,0,1:T(2,128)S(1)} %copy.79), channel_id=1, replica_groups=mesh['depth'=4,'rows'=8] {'rows'}, dimensions={1} | all-to-all | bytes 8388608 | tf_op jit(solution)/shard_map/all_to_all | solution.py:136
  892.5 2.8 copy.80
  895.3 5.3 copy.81
  900.6 8.5 fusion.35
  909.2 0.9 subtract_bitcast_fusion.3
  910.1 0.5 maximum_bitcast_fusion.6
  910.6 9.0 fusion.30
  919.6 6.0 mul.976
  925.6 6.6 copy.85
  (21 shorter events, 1.0 us)
Async XLA Ops:
  109.7 6.1 copy-start
  109.7 190.5 %all-to-all-start = ((f32[8,1,2,512,512]{3,4,2,1,0:T(8,128)}), f32[8,1,2,512,512]{3,4,2,1,0:T(8,128)}, u32[]{:S(2)}, u32[]{:S(2)}) async-start(f32[8,1,2,512,512]{3,4,2,1,0:T(8,128)} %fusion.40), calls=%async_computation | async-start | bytes 33554432 | tf_op jit(solution)/shard_map/all_to_all | solution.py:104
  115.5 719.1 %reduce-scatter.2.cloned.1.call-start = ((), (), s32[]{:S(2)}) async-start(), calls=%async_computation.3 | async-start | bytes 20971520 | tf_op jit(solution)/shard_map/reduce_scatter | solution.py:135
Sparse Core Ops, SparseCore 0:
  553.9 280.6 reduce-scatter.1
